TPU v7x, 32 devices: a whole 2x2x4 slice. The times are simulated.
32 devices in a mesh: gx: 4 (over y, core), gy: 4 (over z), gz: 2 (over x).
Axes of the slice: x: 2, y: 2, z: 4, core: 2. Of those that a mesh axis runs over, the one named last changes fastest.
Arguments:
- heat_level_grid: float32 [64, 256, 512], P('gz', 'gy', 'gx'), may hold values from -16 to 16, as said below
- interval_first_class: int32 [1], replicated, may hold values from 0 to 95
- interval_beyond_class: int32 [1], replicated, may hold values from 128 to 256
Outputs:
- magnitude: float32 [64, 256, 512], P('gz', 'gy', 'gx')
- histogram: float32 [256], replicated
- stats: float32 [4], replicated
Inputs may be any that keep to these rules, and one draw needn't show every extreme that they name: `heat_level_grid`: each entry is a rough value times an amplitude that is constant on blocks of 8 x 4 x 4 cells (z, y, x) and varies over a factor of 16 between blocks.
All inputs are finite; a program needn't handle non-finite values.
Results may differ from a plain program's by a relative error of at most 0.0003.
Values sent between devices are 32-bit elements; how exact they have to be, the bound alone decides.
A program may use at most 64 MiB of HBM per device.

v0:
```python
import jax
import jax.numpy as jnp
from jax import lax
from jax.sharding import PartitionSpec as P

BINS = 256


stencil_coefficients = (0.8, -0.2, 4.0 / 105.0, -1.0 / 280.0)
grad_range = 12.0


def extended_2(block, sides, width):
    for axis, dim in sides:
        count = lax.axis_size(axis)
        forward = [(i, i + 1) for i in range(count - 1)]
        forward.append((count - 1, 0))
        backward = [(target, source) for source, target in forward]
        low = lax.ppermute(
            lax.slice_in_dim(block, block.shape[dim] - width, None, axis=dim), axis, forward
        )
        high = lax.ppermute(lax.slice_in_dim(block, 0, width, axis=dim), axis, backward)
        block = jnp.concatenate([low, block, high], axis=dim)
    return block


def directional_rate(extended, direction_length_count):
    length = extended.shape[direction_length_count] - 8
    running = jnp.zeros(
        extended.shape[:direction_length_count]
        + (length,)
        + extended.shape[direction_length_count + 1 :],
        jnp.float32,
    )
    for offset, coefficient in enumerate(stencil_coefficients, start=1):
        forward_cells = lax.slice_in_dim(
            extended, 4 + offset, 4 + offset + length, axis=direction_length_count
        )
        backward_cells = lax.slice_in_dim(
            extended, 4 - offset, 4 - offset + length, axis=direction_length_count
        )
        running = running + coefficient * (forward_cells - backward_cells)
    return running


def local_counts(low_bin, fraction):
    cell_count = low_bin.shape[0]
    span_cells = min(cell_count, 32768)
    turn_count = cell_count // span_cells
    coarse_rows = BINS // 16
    coarse_ids = jnp.arange(coarse_rows, dtype=jnp.int32)[:, None]
    finer_ids = jnp.arange(16, dtype=jnp.int32)[:, None]

    def one_turn(turn_index, running):
        start = turn_index * span_cells
        low_part = lax.dynamic_slice_in_dim(low_bin, start, span_cells)
        frac_part = lax.dynamic_slice_in_dim(fraction, start, span_cells)
        high_part = low_part + 1
        coarse = jnp.concatenate([low_part // 16, high_part // 16])
        finer = jnp.concatenate([low_part % 16, high_part % 16])
        weight = jnp.concatenate([1.0 - frac_part, frac_part])
        left_side = jnp.where(coarse[None, :] == coarse_ids, weight[None, :], 0.0)
        right_side = (finer[None, :] == finer_ids).astype(jnp.float32)
        product = lax.dot_general(
            left_side,
            right_side,
            (((1,), (1,)), ((), ())),
            precision=lax.Precision.HIGHEST,
            preferred_element_type=jnp.float32,
        )
        return running + product

    running = lax.fori_loop(0, turn_count, one_turn, jnp.zeros((coarse_rows, 16), jnp.float32))
    return running.reshape(BINS)


def on_device(heat_level_grid, interval_first_class, interval_beyond_class):
    grad_x = directional_rate(extended_2(heat_level_grid, (("gx", 2),), 4), 2)
    grad_y = directional_rate(extended_2(heat_level_grid, (("gy", 1),), 4), 1)
    grad_z = directional_rate(extended_2(heat_level_grid, (("gz", 0),), 4), 0)
    slope_norm_square = grad_z * grad_z + grad_y * grad_y + grad_x * grad_x
    magnitude = jnp.sqrt(slope_norm_square + 1.0) - 1.0
    position = jnp.clip(magnitude * (BINS / grad_range), 0.5, BINS - 0.5)
    low_bin = jnp.minimum(jnp.floor(position - 0.5), BINS - 2).astype(jnp.int32)
    fraction = position - 0.5 - low_bin.astype(jnp.float32)
    counts = local_counts(low_bin.reshape(-1), fraction.reshape(-1))
    lower_edge = interval_first_class[0]
    upper_edge = interval_beyond_class[0]
    high_bin = low_bin + 1
    inside_low = (low_bin >= lower_edge) & (low_bin < upper_edge)
    inside_high = (high_bin >= lower_edge) & (high_bin < upper_edge)
    weight = jnp.where(inside_low, 1.0 - fraction, 0.0) + jnp.where(inside_high, fraction, 0.0)
    lowest = jnp.min(magnitude + grad_range * (1.0 - weight))
    highest = jnp.max(weight * magnitude)
    weighted_sum = jnp.sum(weight * magnitude)
    weighted_count = jnp.sum(weight)
    counts, weighted_sum, weighted_count = lax.psum(
        (counts, weighted_sum, weighted_count), ("gx", "gy", "gz")
    )
    highest = lax.pmax(highest, ("gx", "gy", "gz"))
    lowest = lax.pmin(lowest, ("gx", "gy", "gz"))
    total_cells = (
        heat_level_grid.shape[0]
        * heat_level_grid.shape[1]
        * heat_level_grid.shape[2]
        * lax.axis_size("gx")
        * lax.axis_size("gy")
        * lax.axis_size("gz")
    )
    histogram = counts * (BINS / total_cells)
    stats = jnp.stack([lowest, highest, weighted_sum / total_cells, weighted_count / total_cells])
    return (magnitude, histogram, stats)


def solution(mesh):
    return jax.shard_map(
        on_device,
        mesh=mesh,
        in_specs=(P("gz", "gy", "gx"), P(), P()),
        out_specs=(P("gz", "gy", "gx"), P(), P()),
        check_vma=False,
    )
```

profile of v0, /device:TPU:0, one launch (start us, length us, event | category | flops | bytes accessed | tf_op | source)
XLA Modules:
  0.0 196.3 jit_solution(15320877027200136644)
XLA Ops:
  0.6 1.6 fusion.64
  2.3 3.0 %collective-permute-start.1 = (f32[4,64,128]{2,1,0:T(8,128)}, f32[4,64,128]{2,1,0:T(8,128)S(1)}, u32[]{:S(2)}, u32[]{:S(2)}) collective-permute-start(f32[4,64,128]{2,1,0:T(8,128)} %get-tuple-element.251), channel_id=1, source_target_pairs={{0,1},{1,0},{2,3},{3,2},{4,5},{5,4},{6,7},{7,6},{8,9},{9,8},{10,11... | collective-permute-start | bytes 393224 | tf_op jit(solution)/shard_map/ppermute | solution.py:19
  5.3 2.0 %fusion.66 = (f32[32,64,4]{2,1,0:T(8,128)S(1)}, f32[32,64,4]{2,1,0:T(8,128)S(1)}) fusion(f32[32,64,128]{2,1,0:T(8,128)} %param.5), kind=kLoop, calls=%fused_computation.121 | loop fusion | bytes 131072 | tf_op jit(solution)/shard_map/slice | solution.py:22
  7.3 1.0 copy.10
  8.3 0.9 collective-permute-start.4
  9.2 0.4 copy.11
  9.6 0.0 collective-permute-start.5
  9.6 0.7 fusion.65
  10.3 3.7 %collective-permute-start.2 = (f32[32,4,128]{2,1,0:T(4,128)}, f32[32,4,128]{2,1,0:T(4,128)}, u32[]{:S(2)}, u32[]{:S(2)}) collective-permute-start(f32[32,4,128]{2,1,0:T(4,128)} %get-tuple-element.255), channel_id=1, source_target_pairs={{2,0},{4,2},{6,4},{0,6},{3,1},{5,3},{7,5},{1,7},{10,8},{12,10},{14... | collective-permute-start | bytes 196616 | tf_op jit(solution)/shard_map/ppermute | solution.py:22
  15.3 0.1 collective-permute-start.3
  15.4 0.4 copy.7
  15.8 1.2 copy.9
  17.1 0.4 constant_dynamic-update-slice_fusion.1
  17.5 0.9 constant_dynamic-update-slice_fusion.4
  18.3 4.0 %collective-permute-done.3 = f32[32,4,128]{2,1,0:T(4,128)} collective-permute-done((f32[32,4,128]{2,1,0:T(4,128)}, f32[32,4,128]{2,1,0:T(4,128)}, u32[]{:S(2)}, u32[]{:S(2)}) %collective-permute-start.3) | collective-permute-done | bytes 65568 | tf_op jit(solution)/shard_map/ppermute | solution.py:19
  22.3 6.2 %add_reduce_fusion = (f32[]{:T(128)}, f32[]{:T(128)}, f32[]{:T(128)}, f32[]{:T(128)}, f32[32,64,128]{2,1,0:T(8,128)S(1)}) fusion(s32[]{:T(128)} %bitcast.12, s32[]{:T(128)} %bitcast.11, f32[32,64,128]{2,1,0:T(8,128)S(1)} %copy-done, f32[32,64,4]{2,1,0:T(8,128)S(1)} %copy.9, f32[32,64,4]{2,1,0:T(8,128)S(1)} %copy.7, ...), kind=kLoop, calls=%fused_computation.103 | loop fusion | flops 20709376 | bytes 14811160 | tf_op jit(solution)/shard_map/reduce_min | solution.py:93
  28.5 1.4 convert_subtract_fusion
  29.9 43.6 %while.18 = (s32[]{:T(128)}, f32[16,16]{1,0:T(8,128)S(1)}, s32[262144]{0:T(1024)S(1)}, f32[262144]{0:T(1024)}, s32[]{:T(128)}, /*index=5*/s32[]{:T(128)}, s32[]{:T(128)}, s32[]{:T(128)}) while((s32[]{:T(128)}, f32[16,16]{1,0:T(8,128)S(1)}, s32[262144]{0:T(1024)S(1)}, f32[262144]{0:T(1024)}, s32[]{:T(128)}, ...), condition=%wide.region_1.2_spmd.clone.clone, body=%wide.region_0.1_spmd.clone.clone.sunk | while | flops 206176768 | bytes 5703833 | solution.py:73
  29.9 0.1 add_select_fusion.6
  30.0 0.2 add_select_fusion.7
  30.3 0.5 iota_compare_fusion.11
  30.8 0.9 broadcast_subtract_fusion.2
  31.8 3.6 %fusion.76 = f32[16,16]{1,0:T(8,128)S(1)} fusion(f32[65536]{0:T(1024)S(1)} %pad_maximum_fusion.6, s32[65536]{0:T(1024)S(1)} %get-tuple-element.300, f32[16,16]{1,0:T(8,128)S(1)} %get-tuple-element.311, pred[]{:T(512)S(6)} %compare.29, pred[16,65536]{1,0:T(8,128)(4,1)S(1)} %iota_compare_fusion.11), kind=kOutput, calls=%fused_computation.9.clone.3 | convolution fusion | flops 203424256 | bytes 1574913 | tf_op jit(solution)/shard_map/while/body/eval_jaxpr/dot_general | solution.py:64
  35.4 0.1 add_select_fusion.6
  35.5 0.2 add_select_fusion.7
  35.7 0.5 iota_compare_fusion.11
  36.3 0.9 broadcast_subtract_fusion.2
  37.2 3.6 %fusion.76 = f32[16,16]{1,0:T(8,128)S(1)} fusion(f32[65536]{0:T(1024)S(1)} %pad_maximum_fusion.6, s32[65536]{0:T(1024)S(1)} %get-tuple-element.300, f32[16,16]{1,0:T(8,128)S(1)} %get-tuple-element.311, pred[]{:T(512)S(6)} %compare.29, pred[16,65536]{1,0:T(8,128)(4,1)S(1)} %iota_compare_fusion.11), kind=kOutput, calls=%fused_computation.9.clone.3 | convolution fusion | flops 203424256 | bytes 1574913 | tf_op jit(solution)/shard_map/while/body/eval_jaxpr/dot_general | solution.py:64
  40.8 0.1 add_select_fusion.6
  40.9 0.2 add_select_fusion.7
  41.2 0.5 iota_compare_fusion.11
  41.7 0.9 broadcast_subtract_fusion.2
  42.7 3.6 %fusion.76 = f32[16,16]{1,0:T(8,128)S(1)} fusion(f32[65536]{0:T(1024)S(1)} %pad_maximum_fusion.6, s32[65536]{0:T(1024)S(1)} %get-tuple-element.300, f32[16,16]{1,0:T(8,128)S(1)} %get-tuple-element.311, pred[]{:T(512)S(6)} %compare.29, pred[16,65536]{1,0:T(8,128)(4,1)S(1)} %iota_compare_fusion.11), kind=kOutput, calls=%fused_computation.9.clone.3 | convolution fusion | flops 203424256 | bytes 1574913 | tf_op jit(solution)/shard_map/while/body/eval_jaxpr/dot_general | solution.py:64
  46.3 0.1 add_select_fusion.6
  46.4 0.2 add_select_fusion.7
  46.6 0.5 iota_compare_fusion.11
  47.2 0.9 broadcast_subtract_fusion.2
  48.1 3.6 %fusion.76 = f32[16,16]{1,0:T(8,128)S(1)} fusion(f32[65536]{0:T(1024)S(1)} %pad_maximum_fusion.6, s32[65536]{0:T(1024)S(1)} %get-tuple-element.300, f32[16,16]{1,0:T(8,128)S(1)} %get-tuple-element.311, pred[]{:T(512)S(6)} %compare.29, pred[16,65536]{1,0:T(8,128)(4,1)S(1)} %iota_compare_fusion.11), kind=kOutput, calls=%fused_computation.9.clone.3 | convolution fusion | flops 203424256 | bytes 1574913 | tf_op jit(solution)/shard_map/while/body/eval_jaxpr/dot_general | solution.py:64
  51.7 0.1 add_select_fusion.6
  51.8 0.2 add_select_fusion.7
  52.1 0.5 iota_compare_fusion.11
  52.6 0.9 broadcast_subtract_fusion.2
  53.6 3.6 %fusion.76 = f32[16,16]{1,0:T(8,128)S(1)} fusion(f32[65536]{0:T(1024)S(1)} %pad_maximum_fusion.6, s32[65536]{0:T(1024)S(1)} %get-tuple-element.300, f32[16,16]{1,0:T(8,128)S(1)} %get-tuple-element.311, pred[]{:T(512)S(6)} %compare.29, pred[16,65536]{1,0:T(8,128)(4,1)S(1)} %iota_compare_fusion.11), kind=kOutput, calls=%fused_computation.9.clone.3 | convolution fusion | flops 203424256 | bytes 1574913 | tf_op jit(solution)/shard_map/while/body/eval_jaxpr/dot_general | solution.py:64
  57.2 0.1 add_select_fusion.6
  57.3 0.2 add_select_fusion.7
  57.5 0.5 iota_compare_fusion.11
  58.1 0.9 broadcast_subtract_fusion.2
  59.0 3.6 %fusion.76 = f32[16,16]{1,0:T(8,128)S(1)} fusion(f32[65536]{0:T(1024)S(1)} %pad_maximum_fusion.6, s32[65536]{0:T(1024)S(1)} %get-tuple-element.300, f32[16,16]{1,0:T(8,128)S(1)} %get-tuple-element.311, pred[]{:T(512)S(6)} %compare.29, pred[16,65536]{1,0:T(8,128)(4,1)S(1)} %iota_compare_fusion.11), kind=kOutput, calls=%fused_computation.9.clone.3 | convolution fusion | flops 203424256 | bytes 1574913 | tf_op jit(solution)/shard_map/while/body/eval_jaxpr/dot_general | solution.py:64
  62.6 0.1 add_select_fusion.6
  62.7 0.2 add_select_fusion.7
  63.0 0.5 iota_compare_fusion.11
  63.5 0.9 broadcast_subtract_fusion.2
  64.5 3.6 %fusion.76 = f32[16,16]{1,0:T(8,128)S(1)} fusion(f32[65536]{0:T(1024)S(1)} %pad_maximum_fusion.6, s32[65536]{0:T(1024)S(1)} %get-tuple-element.300, f32[16,16]{1,0:T(8,128)S(1)} %get-tuple-element.311, pred[]{:T(512)S(6)} %compare.29, pred[16,65536]{1,0:T(8,128)(4,1)S(1)} %iota_compare_fusion.11), kind=kOutput, calls=%fused_computation.9.clone.3 | convolution fusion | flops 203424256 | bytes 1574913 | tf_op jit(solution)/shard_map/while/body/eval_jaxpr/dot_general | solution.py:64
  68.1 0.1 add_select_fusion.6
  68.2 0.2 add_select_fusion.7
  68.4 0.5 iota_compare_fusion.11
  69.0 0.9 broadcast_subtract_fusion.2
  69.9 3.6 %fusion.76 = f32[16,16]{1,0:T(8,128)S(1)} fusion(f32[65536]{0:T(1024)S(1)} %pad_maximum_fusion.6, s32[65536]{0:T(1024)S(1)} %get-tuple-element.300, f32[16,16]{1,0:T(8,128)S(1)} %get-tuple-element.311, pred[]{:T(512)S(6)} %compare.29, pred[16,65536]{1,0:T(8,128)(4,1)S(1)} %iota_compare_fusion.11), kind=kOutput, calls=%fused_computation.9.clone.3 | convolution fusion | flops 203424256 | bytes 1574913 | tf_op jit(solution)/shard_map/while/body/eval_jaxpr/dot_general | solution.py:64
  73.5 0.1 reshape.20
  73.6 37.5 %all-reduce = (f32[256]{0:T(256)S(1)}, f32[]{:T(128)}, f32[]{:T(128)}) all-reduce(f32[256]{0:T(256)S(1)} %reshape.20, f32[]{:T(128)} %get-tuple-element.224, f32[]{:T(128)} %get-tuple-element.225), channel_id=1, replica_groups=mesh['gx'=4,'gy'=4,'gz'=2] {'gx','gy','gz'}, use_global_device_ids=true, to_apply=%region_2.3 | all-reduce | flops 258 | bytes 2064 | tf_op jit(solution)/shard_map/psum | solution.py:97
  112.4 42.3 %pmax.7 = f32[1]{0:T(128)} all-reduce(f32[1]{0:T(128)} %bitcast.5), channel_id=1, replica_groups=mesh['gx'=4,'gy'=4,'gz'=2] {'gx','gy','gz'}, use_global_device_ids=true, to_apply=%region_6.7 | all-reduce | flops 1 | bytes 8 | tf_op jit(solution)/shard_map/pmax | solution.py:100
  154.7 39.2 %pmin.7 = f32[1]{0:T(128)} all-reduce(f32[1]{0:T(128)} %bitcast.4), channel_id=1, replica_groups=mesh['gx'=4,'gy'=4,'gz'=2] {'gx','gy','gz'}, use_global_device_ids=true, to_apply=%region_4.5 | all-reduce | flops 1 | bytes 8 | tf_op jit(solution)/shard_map/pmin | solution.py:101
  193.9 0.6 broadcast_multiply_fusion
  194.4 1.9 pad_maximum_fusion.4
  (29 shorter events, 0.5 us)
Async XLA Ops:
  2.3 14.8 %collective-permute-start.1 = (f32[4,64,128]{2,1,0:T(8,128)}, f32[4,64,128]{2,1,0:T(8,128)S(1)}, u32[]{:S(2)}, u32[]{:S(2)}) collective-permute-start(f32[4,64,128]{2,1,0:T(8,128)} %get-tuple-element.251), channel_id=1, source_target_pairs={{0,1},{1,0},{2,3},{3,2},{4,5},{5,4},{6,7},{7,6},{8,9},{9,8},{10,11... | collective-permute-start | bytes 393224 | tf_op jit(solution)/shard_map/ppermute | solution.py:19
  5.2 12.2 %collective-permute-start = (f32[4,64,128]{2,1,0:T(8,128)S(1)}, f32[4,64,128]{2,1,0:T(8,128)S(1)}, u32[]{:S(2)}, u32[]{:S(2)}) collective-permute-start(f32[4,64,128]{2,1,0:T(8,128)S(1)} %get-tuple-element.250), channel_id=1, source_target_pairs={{1,0},{0,1},{3,2},{2,3},{5,4},{4,5},{7,6},{6,7},{9,8},{8,9},{11,10... | collective-permute-start | bytes 393224 | tf_op jit(solution)/shard_map/ppermute | solution.py:22
  7.3 2.3 %copy-start = (f32[32,64,128]{2,1,0:T(8,128)S(1)}, f32[32,64,128]{2,1,0:T(8,128)}, u32[]{:S(2)}) copy-start(f32[32,64,128]{2,1,0:T(8,128)} %param.5) | copy-start | bytes 3145732
  8.3 7.0 %collective-permute-start.4 = (f32[32,64,4]{1,0,2:T(8,128)}, f32[32,64,4]{1,0,2:T(8,128)S(1)}, u32[]{:S(2)}, u32[]{:S(2)}) collective-permute-start(f32[32,64,4]{1,0,2:T(8,128)} %copy.10), channel_id=1, source_target_pairs={{8,0},{16,8},{24,16},{0,24},{9,1},{17,9},{25,17},{1,25},{10,2},{18... | collective-permute-start | bytes 98312 | tf_op jit(solution)/shard_map/ppermute | solution.py:22
  9.6 6.2 %collective-permute-start.5 = (f32[32,64,4]{1,0,2:T(8,128)S(1)}, f32[32,64,4]{1,0,2:T(8,128)}, u32[]{:S(2)}, u32[]{:S(2)}) collective-permute-start(f32[32,64,4]{1,0,2:T(8,128)S(1)} %copy.11), channel_id=1, source_target_pairs={{0,8},{8,16},{16,24},{24,0},{1,9},{9,17},{17,25},{25,1},{2,10},{10... | collective-permute-start | bytes 98312 | tf_op jit(solution)/shard_map/ppermute | solution.py:19
  10.3 7.2 %collective-permute-start.2 = (f32[32,4,128]{2,1,0:T(4,128)}, f32[32,4,128]{2,1,0:T(4,128)}, u32[]{:S(2)}, u32[]{:S(2)}) collective-permute-start(f32[32,4,128]{2,1,0:T(4,128)} %get-tuple-element.255), channel_id=1, source_target_pairs={{2,0},{4,2},{6,4},{0,6},{3,1},{5,3},{7,5},{1,7},{10,8},{12,10},{14... | collective-permute-start | bytes 196616 | tf_op jit(solution)/shard_map/ppermute | solution.py:22
  15.3 7.0 %collective-permute-start.3 = (f32[32,4,128]{2,1,0:T(4,128)}, f32[32,4,128]{2,1,0:T(4,128)}, u32[]{:S(2)}, u32[]{:S(2)}) collective-permute-start(f32[32,4,128]{2,1,0:T(4,128)} %get-tuple-element.256), channel_id=1, source_target_pairs={{0,2},{2,4},{4,6},{6,0},{1,3},{3,5},{5,7},{7,1},{8,10},{10,12},{12... | collective-permute-start | bytes 196616 | tf_op jit(solution)/shard_map/ppermute | solution.py:19
  28.5 1.4 copy-start.1
where the time goes:
time: 197 us; the launch traced here: 196 us
  blocking collectives  119 us (60%)
  matrix products  28.5 us (14%)
  other arithmetic  24.5 us (12%)
  local copies, waits for them, and re-layouts  8.67 us (4%)
  starting transfers between devices  7.7 us (4%)
  waiting for transfers between devices  4 us (2%)
  between operations  3.36 us (2%)
    pmax x1, blocking collectives, on_device(): highest = lax.pmax(highest, ('gx', 'gy', 'gz'))  42.3 us
    pmin x1, blocking collectives, on_device(): lowest = lax.pmin(lowest, ('gx', 'gy', 'gz'))  39.2 us
    psum x1, blocking collectives, on_device(): lax.psum((counts, weighted_sum, weighted_count), ('gx', 'gy', 'gz'))  37.5 us
    dot_general x8, matrix products, one_turn(): lax.dot_general(left_side, right_side, (((1,), (1,)), ((), ())), precisio...  28.5 us
    sub x8, other arithmetic, one_turn(): weight = jnp.concatenate([1.0 - frac_part, frac_part])  7.43 us
    reduce_min x1, other arithmetic, on_device(): lowest = jnp.min(magnitude + grad_range * (1.0 - weight))  6.2 us
    ppermute x3, starting transfers between devices, extended_2(): lax.ppermute(lax.slice_in_dim(block, 0, width, axis=dim), axis, backward)  4.62 us
    dot_general x8, other arithmetic, one_turn(): lax.dot_general(left_side, right_side, (((1,), (1,)), ((), ())), precisio...  4.36 us
  transfers between devices with their start and end apart: 6, of which 1 were waited for; matrix products, arithmetic and copies ran while one was open for 4% of the time, Pallas kernels for 0%

commit v1 on v0

v1 whole, which is shorter than its diff:
```python
import functools

import jax
import jax.numpy as jnp
from jax import lax
from jax.experimental import pallas as pl
from jax.experimental.pallas import tpu as pltpu
from jax.sharding import PartitionSpec as P

BINS = 256
FINE = 32
COARSE = BINS // FINE
GROUPS = 8
RANGE = 12.0
COEFS = (0.8, -0.2, 4.0 / 105.0, -1.0 / 280.0)
SCALE = 840.0
TAPS = (672.0, -168.0, 32.0, -3.0)
MESH = pl.DeviceIdType.MESH
F32 = jnp.float32
BF16 = jnp.bfloat16
UNROLL = 2


def tap(distance):
    value = jnp.zeros(distance.shape, F32)
    for k, t in enumerate(TAPS, start=1):
        value = jnp.where(distance == k, t, value)
        value = jnp.where(distance == -k, -t, value)
    return value


def kernel(
    sizes,
    first_ref,
    beyond_ref,
    x_ref,
    mag_ref,
    hist_ref,
    stat_ref,
    ext,
    mag,
    packed,
    from_left,
    from_right,
    band,
    rim_band,
    rim_part,
    acc,
    gather,
    in_sem,
    out_sem,
    send_sem,
    recv_sem,
    ready_y,
    ready_z,
    all_send,
    all_recv,
):
    names = ("gx", "gy", "gz")
    nz, ny, nx = x_ref.shape
    where = {a: lax.axis_index(a) for a in names}
    total = sizes["gx"] * sizes["gy"] * sizes["gz"]

    loads = [
        pltpu.make_async_copy(
            x_ref.at[pl.ds(a, b)], ext.at[pl.ds(4 + a, b), pl.ds(8, ny)], in_sem.at[i]
        )
        for i, (a, b) in enumerate(((0, nz // 2), (nz // 2, nz - nz // 2)))
    ]
    for c in loads:
        c.start()

    def others(axis):
        n = sizes[axis]
        return [lax.rem(where[axis] + d, n) for d in range(1, n)]

    barrier = pltpu.get_barrier_semaphore()
    greeted = 0
    for a in names:
        for other in others(a):
            pl.semaphore_signal(barrier, inc=1, device_id={a: other}, device_id_type=MESH)
            greeted += 1

    row = lax.broadcasted_iota(jnp.int32, (128, 128), 0)
    col = lax.broadcasted_iota(jnp.int32, (128, 128), 1)
    diag = tap(row - col).astype(BF16)
    band[0:128, :] = diag
    band[128:256, :] = diag
    r16 = lax.broadcasted_iota(jnp.int32, (16, 128), 0)
    l16 = lax.broadcasted_iota(jnp.int32, (16, 128), 1)
    m16 = lax.rem(r16, 8)
    place = jnp.where(m16 < 4, m16 - 4, 124 + m16)
    rim_tap = tap(place - l16)
    even = jnp.where(r16 < 8, rim_tap, 0.0).astype(BF16)
    odd = jnp.where(r16 >= 8, rim_tap, 0.0).astype(BF16)
    rim_band[...] = jnp.zeros(rim_band.shape, BF16)
    for j in range(16):
        tile = odd if j % 2 else even
        base = (j // 2) * 16
        rim_band[base : base + 16, 128 * j : 128 * (j + 1)] = tile
        rim_band[128 + base : 144 + base, 128 * j : 128 * (j + 1)] = tile
    acc[...] = jnp.zeros(acc.shape, F32)

    for c in loads:
        c.wait()

    planes = nz // 16
    lane = lax.broadcasted_iota(jnp.int32, (128, 128), 1)
    rims = None
    for j in range(16):
        block = ext[4 + planes * j : 4 + planes * (j + 1), 8 : 8 + ny, :].reshape(planes * ny, 128)
        turned = pltpu.roll(block, (8 * j + 4) % 128, 1)
        rims = turned if rims is None else jnp.where(lane >= 8 * j, turned, rims)
    packed[...] = rims

    pl.semaphore_wait(barrier, greeted)

    def up(a):
        return {a: lax.rem(where[a] + 1, sizes[a])}

    def down(a):
        return {a: lax.rem(where[a] + sizes[a] - 1, sizes[a])}

    def remote(src, dst, i, device):
        return pltpu.make_async_remote_copy(
            src_ref=src,
            dst_ref=dst,
            send_sem=send_sem.at[i],
            recv_sem=recv_sem.at[i],
            device_id=device,
            device_id_type=MESH,
        )

    own = pl.ds(4, nz)
    wide = pl.ds(8, ny)
    z_low = remote(ext.at[pl.ds(nz, 4), wide], ext.at[pl.ds(0, 4), wide], 4, up("gz"))
    z_high = remote(ext.at[pl.ds(4, 4), wide], ext.at[pl.ds(nz + 4, 4), wide], 5, down("gz"))
    y_low = remote(ext.at[own, pl.ds(4 + ny, 4)], ext.at[own, pl.ds(4, 4)], 2, up("gy"))
    y_high = remote(ext.at[own, pl.ds(8, 4)], ext.at[own, pl.ds(8 + ny, 4)], 3, down("gy"))
    x_low = remote(packed, from_left, 0, up("gx"))
    x_high = remote(packed, from_right, 1, down("gx"))
    x_low.start()
    x_high.start()
    y_low.start()
    y_high.start()
    z_low.start()
    z_high.start()
    for other in others("gy"):
        pl.semaphore_signal(ready_y, inc=1, device_id={"gy": other}, device_id_type=MESH)

    x_low.wait()
    x_high.wait()
    rim = jnp.where(lax.rem(lane, 8) < 4, from_left[...], from_right[...])
    rim_hi = rim.astype(BF16)
    rim_lo = (rim - rim_hi.astype(F32)).astype(BF16)
    rim_part[...] = jnp.dot(
        jnp.concatenate([rim_hi, rim_lo], axis=1), rim_band[...], preferred_element_type=F32
    )
    y_low.wait()
    y_high.wait()

    lower = first_ref[0].astype(F32) - 1.0
    upper = beyond_ref[0].astype(F32)
    parity = jnp.where(lax.broadcasted_iota(jnp.int32, (16, 128), 0) >= 8, 1.0, 0.0)

    def twice(a):
        return jnp.concatenate([a, a], axis=0)

    def plane(z):
        here = ext[z + 4, 8 : 8 + ny, :]
        hi = here.astype(BF16)
        lo = (here - hi.astype(F32)).astype(BF16)
        gx = jnp.dot(jnp.concatenate([hi, lo], axis=1), band[...], preferred_element_type=F32)
        rows = pl.multiple_of(lax.rem(z, planes) * ny, ny)
        cols = pl.multiple_of((z // planes) * 128, 128)
        gx = (gx + rim_part[pl.ds(rows, ny), pl.ds(cols, 128)]) * (1.0 / SCALE)
        gy = None
        gz = None
        for k, c in enumerate(COEFS, start=1):
            y_term = c * (ext[z + 4, 8 + k : 8 + k + ny, :] - ext[z + 4, 8 - k : 8 - k + ny, :])
            z_term = c * (ext[z + 4 + k, 8 : 8 + ny, :] - ext[z + 4 - k, 8 : 8 + ny, :])
            gy = y_term if gy is None else gy + y_term
            gz = z_term if gz is None else gz + z_term
        m = jnp.sqrt(gz * gz + gy * gy + gx * gx + 1.0) - 1.0
        mag[z] = m
        q = jnp.clip(m * (BINS / RANGE), 0.5, BINS - 0.5) - 0.5
        low = jnp.minimum(jnp.floor(q), BINS - 2.0)
        frac = q - low
        w = jnp.clip(jnp.minimum(q - lower, upper - q), 0.0, 1.0)
        wm = w * m
        worst = m + RANGE * (1.0 - w)
        coarse = jnp.floor(low * (1.0 / FINE))
        fine = low - FINE * coarse
        frac_hi = frac.astype(BF16).astype(F32)
        frac_lo = frac - frac_hi
        left, right = [], []
        zero = jnp.zeros((16, 128), BF16)
        one = jnp.ones((16, 128), BF16)
        for i in range(ny // 8):
            s = slice(8 * i, 8 * i + 8)
            c2 = (twice(coarse[s]) - parity).astype(BF16)
            f2 = (twice(fine[s]) - parity).astype(BF16)
            h2 = twice(frac_hi[s]).astype(BF16)
            l2 = twice(frac_lo[s]).astype(BF16)
            ones, his, los = [], [], []
            for j in range(COARSE // 2):
                hit = c2 == jnp.asarray(2 * j, BF16)
                ones.append(jnp.where(hit, one, zero))
                his.append(jnp.where(hit, h2, zero))
                los.append(jnp.where(hit, l2, zero))
            left.append(jnp.concatenate(ones + his + los, axis=0))
            right.append(
                jnp.concatenate(
                    [jnp.where(f2 == jnp.asarray(2 * j, BF16), one, zero) for j in range(FINE // 2)], axis=0
                )
            )
        fold = lambda op, a: functools.reduce(op, [a[8 * i : 8 * i + 8] for i in range(ny // 8)])
        return left, right, fold(jnp.add, wm), fold(jnp.add, w), fold(jnp.maximum, wm), fold(jnp.minimum, worst)

    def several(zs, carry):
        left, right = [], []
        s, n, hi, lo = carry
        for z in zs:
            l, r, ps, pn, phi, plo = plane(z)
            left += l
            right += r
            s, n, hi, lo = s + ps, n + pn, jnp.maximum(hi, phi), jnp.minimum(lo, plo)
        acc[...] += lax.dot_general(
            jnp.concatenate(left, axis=1),
            jnp.concatenate(right, axis=1),
            (((1,), (1,)), ((), ())),
            preferred_element_type=F32,
        )
        return s, n, hi, lo

    zeros = jnp.zeros((8, 128), F32)
    carry = (zeros, zeros, zeros, jnp.full((8, 128), 3.0e38, F32))
    inner = (nz - 8) // UNROLL
    carry = lax.fori_loop(
        0, inner, lambda t, c: several([4 + t * UNROLL + u for u in range(UNROLL)], c), carry
    )
    z_low.wait()
    z_high.wait()
    pl.semaphore_wait(ready_y, sizes["gy"] - 1)
    for other in others("gz"):
        pl.semaphore_signal(ready_z, inc=1, device_id={"gz": other}, device_id_type=MESH)
    middle = pltpu.make_async_copy(mag.at[pl.ds(4, nz - 8)], mag_ref.at[pl.ds(4, nz - 8)], out_sem.at[0])
    middle.start()

    def edge(t, c):
        z = t * UNROLL
        z = z + (z // 4) * (nz - 8)
        return several([z + u for u in range(UNROLL)], c)

    wsum, wcount, highest, lowest = lax.fori_loop(0, 8 // UNROLL, edge, carry)

    span = COARSE * GROUPS
    rows = lax.broadcasted_iota(jnp.int32, (span, FINE * GROUPS), 0)
    cols = lax.broadcasted_iota(jnp.int32, (span, FINE * GROUPS), 1)
    keep = lax.rem(rows, GROUPS) == lax.rem(cols, GROUPS)

    def by_class(a):
        a = jnp.where(keep, a, 0.0)
        return jnp.sum(a.reshape(COARSE, GROUPS, FINE * GROUPS), axis=1)

    count = by_class(acc[0:span, :])
    part = by_class(acc[span : 2 * span, :] + acc[2 * span : 3 * span, :])
    from_row = lax.broadcasted_iota(jnp.int32, (FINE * GROUPS, 128), 0) // GROUPS
    to_lane = lax.rem(lax.broadcasted_iota(jnp.int32, (FINE * GROUPS, 128), 1), FINE)
    spread = jnp.where(from_row == to_lane, 1.0, 0.0)
    both = jnp.dot(
        jnp.concatenate([count, part], axis=0),
        spread,
        precision=lax.Precision.HIGHEST,
        preferred_element_type=F32,
    )
    r8 = lax.broadcasted_iota(jnp.int32, (16, 128), 0)
    l8 = lax.broadcasted_iota(jnp.int32, (16, 128), 1)
    both = jnp.where(lax.rem(r8, 4) == l8 // FINE, both, 0.0)
    quad = [jnp.sum(both[4 * i : 4 * i + 4], axis=0, keepdims=True) for i in range(4)]
    lane1 = lax.broadcasted_iota(jnp.int32, (1, 128), 1)
    turned = [pltpu.roll(quad[2], 1, 1), pltpu.roll(quad[3], 1, 1)]
    row0 = quad[0] - quad[2] + jnp.where(lane1 == 0, turned[1], turned[0])
    row1 = quad[1] - quad[3] + jnp.where(lane1 == 0, turned[0], turned[1])

    def all_of(op, a):
        return op(op(a, axis=0, keepdims=True), axis=1, keepdims=True)

    row2 = jnp.where(
        lane1 == 0,
        all_of(jnp.min, lowest),
        jnp.where(
            lane1 == 1,
            all_of(jnp.max, highest),
            jnp.where(lane1 == 2, all_of(jnp.sum, wsum), all_of(jnp.sum, wcount)),
        ),
    )
    me = (where["gx"] * sizes["gy"] + where["gy"]) * sizes["gz"] + where["gz"]
    gather[me] = jnp.concatenate([row0, row1, row2, jnp.zeros((1, 128), F32)], axis=0)

    pl.semaphore_wait(ready_z, sizes["gz"] - 1)

    def spread_out(t, c):
        other = lax.rem(me + t, total)
        pltpu.make_async_remote_copy(
            src_ref=gather.at[me],
            dst_ref=gather.at[me],
            send_sem=all_send,
            recv_sem=all_recv,
            device_id={
                "gx": other // (sizes["gy"] * sizes["gz"]),
                "gy": lax.rem(other // sizes["gz"], sizes["gy"]),
                "gz": lax.rem(other, sizes["gz"]),
            },
            device_id_type=MESH,
        ).start()
        return c

    lax.fori_loop(1, total, spread_out, 0)
    outer = [
        pltpu.make_async_copy(mag.at[pl.ds(a, 4)], mag_ref.at[pl.ds(a, 4)], out_sem.at[i])
        for i, a in ((1, 0), (2, nz - 4))
    ]
    for c in outer:
        c.start()
    rest = gather.at[pl.ds(0, total - 1)]
    every = pltpu.make_async_remote_copy(
        src_ref=rest,
        dst_ref=rest,
        send_sem=all_send,
        recv_sem=all_recv,
        device_id=up("gx"),
        device_id_type=MESH,
    )
    every.wait()
    parts = gather[...]
    summed = jnp.sum(parts, axis=0)
    smallest = jnp.min(parts, axis=0)
    largest = jnp.max(parts, axis=0)
    cells = nz * ny * nx * total
    hist_ref[...] = summed[0:2] * (BINS / cells)
    stat_ref[...] = jnp.where(
        lane1 == 0,
        smallest[2:3],
        jnp.where(lane1 == 1, largest[2:3], summed[2:3] * (1.0 / cells)),
    )
    middle.wait()
    for c in outer:
        c.wait()


def solution(mesh):
    sizes = dict(mesh.shape)
    total = sizes["gx"] * sizes["gy"] * sizes["gz"]

    def on_device(grid, first, beyond):
        nz, ny, nx = grid.shape
        vmem = pl.BlockSpec(memory_space=pltpu.VMEM)
        smem = pl.BlockSpec(memory_space=pltpu.SMEM)
        anywhere = pl.BlockSpec(memory_space=pl.ANY)
        packed_rows = nz * ny // 16
        magnitude, histogram, stats = pl.pallas_call(
            functools.partial(kernel, sizes),
            out_shape=(
                jax.ShapeDtypeStruct(grid.shape, F32),
                jax.ShapeDtypeStruct((2, 128), F32),
                jax.ShapeDtypeStruct((1, 128), F32),
            ),
            in_specs=[smem, smem, anywhere],
            out_specs=(anywhere, vmem, vmem),
            scratch_shapes=[
                pltpu.VMEM((nz + 8, ny + 16, nx), F32),
                pltpu.VMEM((nz, ny, nx), F32),
                pltpu.VMEM((packed_rows, 128), F32),
                pltpu.VMEM((packed_rows, 128), F32),
                pltpu.VMEM((packed_rows, 128), F32),
                pltpu.VMEM((256, 128), BF16),
                pltpu.VMEM((256, 2048), BF16),
                pltpu.VMEM((packed_rows, 2048), F32),
                pltpu.VMEM((3 * COARSE * GROUPS, FINE * GROUPS), F32),
                pltpu.VMEM((total, 4, 128), F32),
                pltpu.SemaphoreType.DMA((2,)),
                pltpu.SemaphoreType.DMA((3,)),
                pltpu.SemaphoreType.DMA((6,)),
                pltpu.SemaphoreType.DMA((6,)),
                pltpu.SemaphoreType.REGULAR,
                pltpu.SemaphoreType.REGULAR,
                pltpu.SemaphoreType.DMA,
                pltpu.SemaphoreType.DMA,
            ],
            compiler_params=pltpu.CompilerParams(
                collective_id=0, has_side_effects=True, vmem_limit_bytes=32 * 1024 * 1024
            ),
        )(first, beyond, grid)
        return magnitude, histogram.reshape(BINS), stats[0, 0:4]

    return jax.shard_map(
        on_device,
        mesh=mesh,
        in_specs=(P("gz", "gy", "gx"), P(), P()),
        out_specs=(P("gz", "gy", "gx"), P(), P()),
        check_vma=False,
    )
```

time: 197 us -> 33.5 us (0.17)
  blocking collectives: 119 us -> 0 us
  matrix products: 28.5 us -> 0 us
  Pallas kernels: 0 us -> 28.1 us
  other arithmetic: 24.5 us -> 0 us
  starting transfers between devices: 7.7 us -> 0 us
  local copies, waits for them, and re-layouts: 8.67 us -> 3.26 us
  waiting for transfers between devices: 4 us -> 0 us
    pmax x1 -> x0, blocking collectives: 42.3 us -> none  [on_device(): highest = lax.pmax(highest, ('gx', 'gy', 'gz'))]
    pmin x1 -> x0, blocking collectives: 39.2 us -> none  [on_device(): lowest = lax.pmin(lowest, ('gx', 'gy', 'gz'))]
    psum x1 -> x0, blocking collectives: 37.5 us -> none  [on_device(): lax.psum((counts, weighted_sum, weighted_count), ('gx', 'gy', 'gz'))]
    dot_general x8 -> x0, matrix products: 28.5 us -> none  [one_turn(): lax.dot_general(left_side, right_side, (((1,), (1,)), ((), ())), precisio...]
    pallas_call x0 -> x1, Pallas kernels: none -> 28.1 us  [on_device(): pl.pallas_call(functools.partial(kernel, sizes), out_shape=(jax.ShapeDtyp...]
    sub x9 -> x0, other arithmetic: 8.82 us -> none  [the longest x8 7.43 us: one_turn(): weight = jnp.concatenate([1.0 - frac_part, frac_part])]
    ppermute x6 -> x0, starting transfers between devices: 7.7 us -> none  [the longest x3 4.62 us: extended_2(): lax.ppermute(lax.slice_in_dim(block, 0, width, axis=dim), axis, backward)]
    reduce_min x1 -> x0, other arithmetic: 6.2 us -> none  [on_device(): lowest = jnp.min(magnitude + grad_range * (1.0 - weight))]
  transfers between devices with their start and end apart: 6 -> 0, of which waited for: 1 -> 0; matrix products, arithmetic and copies ran while one was open for 4% -> 0% of each run, Pallas kernels for 0% -> 0%
where the time goes in v1:
time: 33.5 us; the launch traced here: 33.3 us
  Pallas kernels  28.1 us (84%)
  local copies, waits for them, and re-layouts  3.26 us (10%)
  between operations  1.94 us (6%)
    pallas_call x1, Pallas kernels, on_device(): pl.pallas_call(functools.partial(kernel, sizes), out_shape=(jax.ShapeDtyp...  28.1 us
    unnamed x4, local copies, waits for them, and re-layouts  2.75 us

profile of v1, /device:TPU:0, one launch (start us, length us, event | category | flops | bytes accessed | tf_op | source)
XLA Modules:
  0.0 33.3 jit_solution(7389385124780856115)
XLA Ops:
  1.9 0.0 copy-start
  1.9 1.2 %copy-done = f32[32,64,128]{2,1,0:T(8,128)S(1)} copy-done((f32[32,64,128]{2,1,0:T(8,128)S(1)}, f32[32,64,128]{2,1,0:T(8,128)}, u32[]{:S(2)}) %copy-start) | copy-done | bytes 1048600
  3.1 28.1 %shard_map.58 = (f32[32,64,128]{2,1,0:T(8,128)S(1)}, f32[2,128]{1,0:T(2,128)S(1)}, f32[1,128]{1,0:T(1,128)S(1)}) custom-call(s32[1]{0:T(128)S(6)} %copy.8.first_ref, s32[1]{0:T(128)S(6)} %copy.9.beyond_ref, f32[32,64,128]{2,1,0:T(8,128)S(1)} %copy-done), custom_call_target="tpu_custom_call" | custom-call | tf_op jit(solution)/shard_map/pallas_call | solution.py:362
  31.3 0.5 %slice_bitcast_fusion = f32[4]{0:T(128)} fusion(f32[1,128]{1,0:T(1,128)S(1)} %get-tuple-element.8), kind=kLoop, calls=%fused_computation | loop fusion | bytes 32 | tf_op jit(solution)/shard_map/squeeze | solution.py:395
  31.8 1.0 %copy.10 = f32[32,64,128]{2,1,0:T(8,128)} copy(f32[32,64,128]{2,1,0:T(8,128)S(1)} %get-tuple-element.12) | data formatting | bytes 2097152
  32.8 0.6 %copy.11 = f32[256]{0:T(256)} copy(f32[256]{0:T(256)S(1)} %bitcast.3) | data formatting | bytes 2048
Async XLA Ops:
  1.9 1.2 %copy-start = (f32[32,64,128]{2,1,0:T(8,128)S(1)}, f32[32,64,128]{2,1,0:T(8,128)}, u32[]{:S(2)}) copy-start(f32[32,64,128]{2,1,0:T(8,128)} %x_ref.1) | copy-start | bytes 3145732

commit v2 on v1

--- a/solution.py
+++ b/solution.py
@@ -18,7 +18,8 @@
 MESH = pl.DeviceIdType.MESH
 F32 = jnp.float32
 BF16 = jnp.bfloat16
-UNROLL = 2
+UNROLL = 4
+EDGE = 2
 
 
 def tap(distance):
@@ -38,7 +39,6 @@
     hist_ref,
     stat_ref,
     ext,
-    mag,
     packed,
     from_left,
     from_right,
@@ -48,7 +48,6 @@
     acc,
     gather,
     in_sem,
-    out_sem,
     send_sem,
     recv_sem,
     ready_y,
@@ -74,6 +73,7 @@
         n = sizes[axis]
         return [lax.rem(where[axis] + d, n) for d in range(1, n)]
 
+    ahead = {(a, d): lax.rem(where[a] + d, sizes[a]) for a in names for d in range(sizes[a])}
     barrier = pltpu.get_barrier_semaphore()
     greeted = 0
     for a in names:
@@ -156,9 +156,6 @@
     rim_part[...] = jnp.dot(
         jnp.concatenate([rim_hi, rim_lo], axis=1), rim_band[...], preferred_element_type=F32
     )
-    y_low.wait()
-    y_high.wait()
-
     lower = first_ref[0].astype(F32) - 1.0
     upper = beyond_ref[0].astype(F32)
     parity = jnp.where(lax.broadcasted_iota(jnp.int32, (16, 128), 0) >= 8, 1.0, 0.0)
@@ -166,23 +163,29 @@
     def twice(a):
         return jnp.concatenate([a, a], axis=0)
 
-    def plane(z):
-        here = ext[z + 4, 8 : 8 + ny, :]
-        hi = here.astype(BF16)
-        lo = (here - hi.astype(F32)).astype(BF16)
-        gx = jnp.dot(jnp.concatenate([hi, lo], axis=1), band[...], preferred_element_type=F32)
-        rows = pl.multiple_of(lax.rem(z, planes) * ny, ny)
+    def rates(blocks):
+        sides = []
+        for z, t0, nt in blocks:
+            here = ext[z + 4, 8 + 8 * t0 : 8 + 8 * (t0 + nt), :]
+            hi = here.astype(BF16)
+            lo = (here - hi.astype(F32)).astype(BF16)
+            sides.append(jnp.concatenate([hi, lo], axis=1))
+        return jnp.dot(jnp.concatenate(sides, axis=0), band[...], preferred_element_type=F32)
+
+    def plane(z, t0, nt, gx):
+        y0, n = 8 + 8 * t0, 8 * nt
+        rows = pl.multiple_of(lax.rem(z, planes) * ny + 8 * t0, 8)
         cols = pl.multiple_of((z // planes) * 128, 128)
-        gx = (gx + rim_part[pl.ds(rows, ny), pl.ds(cols, 128)]) * (1.0 / SCALE)
+        gx = (gx + rim_part[pl.ds(rows, n), pl.ds(cols, 128)]) * (1.0 / SCALE)
         gy = None
         gz = None
         for k, c in enumerate(COEFS, start=1):
-            y_term = c * (ext[z + 4, 8 + k : 8 + k + ny, :] - ext[z + 4, 8 - k : 8 - k + ny, :])
-            z_term = c * (ext[z + 4 + k, 8 : 8 + ny, :] - ext[z + 4 - k, 8 : 8 + ny, :])
+            y_term = c * (ext[z + 4, y0 + k : y0 + k + n, :] - ext[z + 4, y0 - k : y0 - k + n, :])
+            z_term = c * (ext[z + 4 + k, y0 : y0 + n, :] - ext[z + 4 - k, y0 : y0 + n, :])
             gy = y_term if gy is None else gy + y_term
             gz = z_term if gz is None else gz + z_term
         m = jnp.sqrt(gz * gz + gy * gy + gx * gx + 1.0) - 1.0
-        mag[z] = m
+        mag_ref[z, 8 * t0 : 8 * (t0 + nt), :] = m
         q = jnp.clip(m * (BINS / RANGE), 0.5, BINS - 0.5) - 0.5
         low = jnp.minimum(jnp.floor(q), BINS - 2.0)
         frac = q - low
@@ -196,7 +199,7 @@
         left, right = [], []
         zero = jnp.zeros((16, 128), BF16)
         one = jnp.ones((16, 128), BF16)
-        for i in range(ny // 8):
+        for i in range(nt):
             s = slice(8 * i, 8 * i + 8)
             c2 = (twice(coarse[s]) - parity).astype(BF16)
             f2 = (twice(fine[s]) - parity).astype(BF16)
@@ -214,14 +217,17 @@
                     [jnp.where(f2 == jnp.asarray(2 * j, BF16), one, zero) for j in range(FINE // 2)], axis=0
                 )
             )
-        fold = lambda op, a: functools.reduce(op, [a[8 * i : 8 * i + 8] for i in range(ny // 8)])
+        fold = lambda op, a: functools.reduce(op, [a[8 * i : 8 * i + 8] for i in range(nt)])
         return left, right, fold(jnp.add, wm), fold(jnp.add, w), fold(jnp.maximum, wm), fold(jnp.minimum, worst)
 
-    def several(zs, carry):
+    def several(blocks, carry):
         left, right = [], []
         s, n, hi, lo = carry
-        for z in zs:
-            l, r, ps, pn, phi, plo = plane(z)
+        gx = rates(blocks)
+        start = 0
+        for z, t0, nt in blocks:
+            l, r, ps, pn, phi, plo = plane(z, t0, nt, gx[start : start + 8 * nt])
+            start += 8 * nt
             left += l
             right += r
             s, n, hi, lo = s + ps, n + pn, jnp.maximum(hi, phi), jnp.minimum(lo, plo)
@@ -235,24 +241,29 @@
 
     zeros = jnp.zeros((8, 128), F32)
     carry = (zeros, zeros, zeros, jnp.full((8, 128), 3.0e38, F32))
+    tiles = ny // 8
     inner = (nz - 8) // UNROLL
     carry = lax.fori_loop(
-        0, inner, lambda t, c: several([4 + t * UNROLL + u for u in range(UNROLL)], c), carry
+        0, inner, lambda t, c: several([(4 + t * UNROLL + u, 1, tiles - 2) for u in range(UNROLL)], c), carry
+    )
+    y_low.wait()
+    y_high.wait()
+    ends = [(u, t0, 1) for u in range(8) for t0 in (0, tiles - 1)]
+    carry = lax.fori_loop(
+        0, (nz - 8) // 8, lambda t, c: several([(4 + t * 8 + u, a, b) for u, a, b in ends], c), carry
     )
     z_low.wait()
     z_high.wait()
     pl.semaphore_wait(ready_y, sizes["gy"] - 1)
     for other in others("gz"):
         pl.semaphore_signal(ready_z, inc=1, device_id={"gz": other}, device_id_type=MESH)
-    middle = pltpu.make_async_copy(mag.at[pl.ds(4, nz - 8)], mag_ref.at[pl.ds(4, nz - 8)], out_sem.at[0])
-    middle.start()
 
     def edge(t, c):
-        z = t * UNROLL
+        z = t * EDGE
         z = z + (z // 4) * (nz - 8)
-        return several([z + u for u in range(UNROLL)], c)
-
-    wsum, wcount, highest, lowest = lax.fori_loop(0, 8 // UNROLL, edge, carry)
+        return several([(z + u, 0, tiles) for u in range(EDGE)], c)
+
+    wsum, wcount, highest, lowest = lax.fori_loop(0, 8 // EDGE, edge, carry)
 
     span = COARSE * GROUPS
     rows = lax.broadcasted_iota(jnp.int32, (span, FINE * GROUPS), 0)
@@ -300,29 +311,34 @@
 
     pl.semaphore_wait(ready_z, sizes["gz"] - 1)
 
-    def spread_out(t, c):
-        other = lax.rem(me + t, total)
+    def spread_to(gx, gy, gz):
         pltpu.make_async_remote_copy(
             src_ref=gather.at[me],
             dst_ref=gather.at[me],
             send_sem=all_send,
             recv_sem=all_recv,
-            device_id={
-                "gx": other // (sizes["gy"] * sizes["gz"]),
-                "gy": lax.rem(other // sizes["gz"], sizes["gy"]),
-                "gz": lax.rem(other, sizes["gz"]),
-            },
+            device_id={"gx": gx, "gy": gy, "gz": gz},
             device_id_type=MESH,
         ).start()
+
+    def spread_out(t, c):
+        other = lax.rem(me + t, total)
+        spread_to(
+            other // (sizes["gy"] * sizes["gz"]),
+            lax.rem(other // sizes["gz"], sizes["gy"]),
+            lax.rem(other, sizes["gz"]),
+        )
         return c
 
-    lax.fori_loop(1, total, spread_out, 0)
-    outer = [
-        pltpu.make_async_copy(mag.at[pl.ds(a, 4)], mag_ref.at[pl.ds(a, 4)], out_sem.at[i])
-        for i, a in ((1, 0), (2, nz - 4))
-    ]
-    for c in outer:
-        c.start()
+    if total > 64:
+        lax.fori_loop(1, total, spread_out, 0)
+    else:
+        far = lambda n: sorted(range(n), key=lambda d: -min(d, n - d))
+        for dy in far(sizes["gy"]):
+            for dz in far(sizes["gz"]):
+                for dx in far(sizes["gx"]):
+                    if dx or dy or dz:
+                        spread_to(*[ahead[a, d] for a, d in (("gx", dx), ("gy", dy), ("gz", dz))])
     rest = gather.at[pl.ds(0, total - 1)]
     every = pltpu.make_async_remote_copy(
         src_ref=rest,
@@ -343,10 +359,15 @@
         lane1 == 0,
         smallest[2:3],
         jnp.where(lane1 == 1, largest[2:3], summed[2:3] * (1.0 / cells)),
-    )
-    middle.wait()
-    for c in outer:
-        c.wait()
+    )[:, 0:4]
+
+
+def finish(mag_ref, hist_ref, stat_ref, mag_out, hist_out, stat_out, sem):
+    copy = pltpu.make_async_copy(mag_ref, mag_out, sem)
+    copy.start()
+    hist_out[...] = hist_ref[...]
+    stat_out[...] = stat_ref[...]
+    copy.wait()
 
 
 def solution(mesh):
@@ -356,21 +377,19 @@
     def on_device(grid, first, beyond):
         nz, ny, nx = grid.shape
         vmem = pl.BlockSpec(memory_space=pltpu.VMEM)
-        smem = pl.BlockSpec(memory_space=pltpu.SMEM)
-        anywhere = pl.BlockSpec(memory_space=pl.ANY)
+        hbm = pl.BlockSpec(memory_space=pltpu.HBM)
         packed_rows = nz * ny // 16
         magnitude, histogram, stats = pl.pallas_call(
             functools.partial(kernel, sizes),
             out_shape=(
                 jax.ShapeDtypeStruct(grid.shape, F32),
                 jax.ShapeDtypeStruct((2, 128), F32),
-                jax.ShapeDtypeStruct((1, 128), F32),
+                jax.ShapeDtypeStruct((1, 4), F32),
             ),
-            in_specs=[smem, smem, anywhere],
-            out_specs=(anywhere, vmem, vmem),
+            in_specs=[pl.BlockSpec(memory_space=pltpu.SMEM), pl.BlockSpec(memory_space=pltpu.SMEM), hbm],
+            out_specs=(vmem, vmem, vmem),
             scratch_shapes=[
                 pltpu.VMEM((nz + 8, ny + 16, nx), F32),
-                pltpu.VMEM((nz, ny, nx), F32),
                 pltpu.VMEM((packed_rows, 128), F32),
                 pltpu.VMEM((packed_rows, 128), F32),
                 pltpu.VMEM((packed_rows, 128), F32),
@@ -380,7 +399,6 @@
                 pltpu.VMEM((3 * COARSE * GROUPS, FINE * GROUPS), F32),
                 pltpu.VMEM((total, 4, 128), F32),
                 pltpu.SemaphoreType.DMA((2,)),
-                pltpu.SemaphoreType.DMA((3,)),
                 pltpu.SemaphoreType.DMA((6,)),
                 pltpu.SemaphoreType.DMA((6,)),
                 pltpu.SemaphoreType.REGULAR,
@@ -389,10 +407,22 @@
                 pltpu.SemaphoreType.DMA,
             ],
             compiler_params=pltpu.CompilerParams(
-                collective_id=0, has_side_effects=True, vmem_limit_bytes=32 * 1024 * 1024
+                collective_id=0, has_side_effects=True, vmem_limit_bytes=32768 * 1024
             ),
         )(first, beyond, grid)
-        return magnitude, histogram.reshape(BINS), stats[0, 0:4]
+        magnitude, histogram, stats = pl.pallas_call(
+            finish,
+            out_shape=(
+                jax.ShapeDtypeStruct(grid.shape, F32),
+                jax.ShapeDtypeStruct((2, 128), F32),
+                jax.ShapeDtypeStruct((1, 4), F32),
+            ),
+            in_specs=[vmem, vmem, vmem],
+            out_specs=(hbm, vmem, vmem),
+            scratch_shapes=[pltpu.SemaphoreType.DMA],
+            compiler_params=pltpu.CompilerParams(vmem_limit_bytes=4 * 1024 * 1024),
+        )(magnitude, histogram, stats)
+        return magnitude, histogram.reshape(BINS), stats.reshape(4)
 
     return jax.shard_map(
         on_device,

time: 33.5 us -> 28.9 us (0.86)
  Pallas kernels: 28.1 us -> 25.5 us
  local copies, waits for them, and re-layouts: 3.26 us -> 1.22 us
    pallas_call x1, Pallas kernels: 28.1 us -> 24 us  [on_device(): pl.pallas_call(functools.partial(kernel, sizes), out_shape=(jax.ShapeDtyp...]
    pallas_call x0 -> x1, Pallas kernels: none -> 1.54 us  [on_device(): pl.pallas_call(finish, out_shape=(jax.ShapeDtypeStruct(grid.shape, F32),...]
    unnamed x4 -> x2, local copies, waits for them, and re-layouts: 2.75 us -> 1.22 us
    squeeze x1 -> x0, local copies, waits for them, and re-layouts: 0.51 us -> none  [on_device(): return (magnitude, histogram.reshape(BINS), stats[0, 0:4])]
where the time goes in v2:
time: 28.9 us; the launch traced here: 28.7 us
  Pallas kernels  25.5 us (88%)
  between operations  1.94 us (7%)
  local copies, waits for them, and re-layouts  1.22 us (4%)
    pallas_call x1, Pallas kernels, on_device(): pl.pallas_call(functools.partial(kernel, sizes), out_shape=(jax.ShapeDtyp...  24 us
    pallas_call x1, Pallas kernels, on_device(): pl.pallas_call(finish, out_shape=(jax.ShapeDtypeStruct(grid.shape, F32),...  1.54 us
    unnamed x2, local copies, waits for them, and re-layouts  1.22 us

profile of v2, /device:TPU:0, one launch (start us, length us, event | category | flops | bytes accessed | tf_op | source)
XLA Modules:
  0.0 28.7 jit_solution(7887304524243841190)
XLA Ops:
  1.9 0.0 copy-start
  1.9 1.2 %copy-done = f32[32,64,128]{2,1,0:T(8,128)S(1)} copy-done((f32[32,64,128]{2,1,0:T(8,128)S(1)}, f32[32,64,128]{2,1,0:T(8,128)}, u32[]{:S(2)}) %copy-start) | copy-done | bytes 1048600
  3.1 24.0 %shard_map.58 = (f32[32,64,128]{2,1,0:T(8,128)S(1)}, f32[2,128]{1,0:T(2,128)S(1)}, f32[1,4]{1,0:T(1,128)S(1)}) custom-call(s32[1]{0:T(128)S(6)} %copy.6.first_ref, s32[1]{0:T(128)S(6)} %copy.7.beyond_ref, f32[32,64,128]{2,1,0:T(8,128)S(1)} %copy-done), custom_call_target="tpu_custom_call" | custom-call | tf_op jit(solution)/shard_map/pallas_call | solution.py:382
  27.2 1.5 %shard_map.59 = (f32[32,64,128]{2,1,0:T(8,128)}, f32[2,128]{1,0:T(2,128)}, f32[1,4]{1,0:T(1,128)}) custom-call(f32[32,64,128]{2,1,0:T(8,128)S(1)} %get-tuple-element.9.mag_ref, f32[2,128]{1,0:T(2,128)S(1)} %get-tuple-element.10.hist_ref, f32[1,4]{1,0:T(1,128)S(1)} %get-tuple-element.11.stat_ref), custom_call_target="tpu_custom_call" | custom-call | tf_op jit(solution)/shard_map/pallas_call | solution.py:413
Async XLA Ops:
  1.9 1.2 %copy-start = (f32[32,64,128]{2,1,0:T(8,128)S(1)}, f32[32,64,128]{2,1,0:T(8,128)}, u32[]{:S(2)}) copy-start(f32[32,64,128]{2,1,0:T(8,128)} %x_ref.1) | copy-start | bytes 3145732

commit v3 on v2

--- a/solution.py
+++ b/solution.py
@@ -18,8 +18,8 @@
 MESH = pl.DeviceIdType.MESH
 F32 = jnp.float32
 BF16 = jnp.bfloat16
-UNROLL = 4
-EDGE = 2
+UNROLL = 8
+EDGE = 4
 
 
 def tap(distance):
@@ -248,9 +248,9 @@
     )
     y_low.wait()
     y_high.wait()
-    ends = [(u, t0, 1) for u in range(8) for t0 in (0, tiles - 1)]
+    ends = [(u, t0, 1) for u in range(nz - 8) for t0 in (0, tiles - 1)]
     carry = lax.fori_loop(
-        0, (nz - 8) // 8, lambda t, c: several([(4 + t * 8 + u, a, b) for u, a, b in ends], c), carry
+        0, 1, lambda t, c: several([(4 + t * (nz - 8) + u, a, b) for u, a, b in ends], c), carry
     )
     z_low.wait()
     z_high.wait()

time: 28.9 us -> 27 us (0.934)
  Pallas kernels: 25.5 us -> 23.6 us
    pallas_call x1, Pallas kernels: 24 us -> 22.1 us  [on_device(): pl.pallas_call(functools.partial(kernel, sizes), out_shape=(jax.ShapeDtyp...]
where the time goes in v3:
time: 27 us; the launch traced here: 26.8 us
  Pallas kernels  23.6 us (87%)
  between operations  1.94 us (7%)
  local copies, waits for them, and re-layouts  1.22 us (5%)
    pallas_call x1, Pallas kernels, on_device(): pl.pallas_call(functools.partial(kernel, sizes), out_shape=(jax.ShapeDtyp...  22.1 us
    pallas_call x1, Pallas kernels, on_device(): pl.pallas_call(finish, out_shape=(jax.ShapeDtypeStruct(grid.shape, F32),...  1.54 us
    unnamed x2, local copies, waits for them, and re-layouts  1.22 us

profile of v3, /device:TPU:0, one launch (start us, length us, event | category | flops | bytes accessed | tf_op | source)
XLA Modules:
  0.0 26.8 jit_solution(7220607964221448286)
XLA Ops:
  1.9 0.0 copy-start
  1.9 1.2 %copy-done = f32[32,64,128]{2,1,0:T(8,128)S(1)} copy-done((f32[32,64,128]{2,1,0:T(8,128)S(1)}, f32[32,64,128]{2,1,0:T(8,128)}, u32[]{:S(2)}) %copy-start) | copy-done | bytes 1048600
  3.1 22.1 %shard_map.58 = (f32[32,64,128]{2,1,0:T(8,128)S(1)}, f32[2,128]{1,0:T(2,128)S(1)}, f32[1,4]{1,0:T(1,128)S(1)}) custom-call(s32[1]{0:T(128)S(6)} %copy.6.first_ref, s32[1]{0:T(128)S(6)} %copy.7.beyond_ref, f32[32,64,128]{2,1,0:T(8,128)S(1)} %copy-done), custom_call_target="tpu_custom_call" | custom-call | tf_op jit(solution)/shard_map/pallas_call | solution.py:382
  25.2 1.5 %shard_map.59 = (f32[32,64,128]{2,1,0:T(8,128)}, f32[2,128]{1,0:T(2,128)}, f32[1,4]{1,0:T(1,128)}) custom-call(f32[32,64,128]{2,1,0:T(8,128)S(1)} %get-tuple-element.9.mag_ref, f32[2,128]{1,0:T(2,128)S(1)} %get-tuple-element.10.hist_ref, f32[1,4]{1,0:T(1,128)S(1)} %get-tuple-element.11.stat_ref), custom_call_target="tpu_custom_call" | custom-call | tf_op jit(solution)/shard_map/pallas_call | solution.py:413
Async XLA Ops:
  1.9 1.2 %copy-start = (f32[32,64,128]{2,1,0:T(8,128)S(1)}, f32[32,64,128]{2,1,0:T(8,128)}, u32[]{:S(2)}) copy-start(f32[32,64,128]{2,1,0:T(8,128)} %x_ref.1) | copy-start | bytes 3145732
